TPU v7x, 32 devices: a whole 2x2x4 slice. The times are simulated.
32 devices in a mesh: dp: 4 (over z), head: 2 (over y), tok: 4 (over x, core).
Axes of the slice: x: 2, y: 2, z: 4, core: 2. Of those that a mesh axis runs over, the one named last changes fastest.
Arguments:
- mamba_input: bfloat16 [8, 64, 2048], P('dp', 'tok', 'head'), may hold values from -6 to 6
- gate_input: bfloat16 [8, 64, 2048], P('dp', 'tok', 'head'), may hold values from -6 to 6
- in_b: bfloat16 [8, 64, 256], P('dp', 'tok', 'head'), may hold values from -0.75 to 0.75
- in_c: bfloat16 [8, 64, 256], P('dp', 'tok', 'head'), may hold values from -0.75 to 0.75
- step_size: bfloat16 [8, 64, 32], P('dp', 'tok', 'head'), may hold values from 0.019897461 to 1
- decay_rate: float32 [32], P('head'), may hold values from 0.01 to 1
- skip_weight: float32 [32], P('head'), may hold values from 0.5 to 1.5
- norm_gain: float32 [2048], P('head'), may hold values from 0.1 to 1.9
- ssm_state: bfloat16 [8, 32, 64, 128], P('dp', 'head', None, 'tok'), may hold values from -6 to 6
- out_weight: bfloat16 [2048, 4096], P(('head', 'tok')), may hold values from -0.125 to 0.125
- queries: bfloat16 [8, 64, 1024], P('dp', 'tok', 'head'), may hold values from -6 to 6
- draft_token_keys: bfloat16 [8, 64, 256], P('dp', 'tok', 'head'), may hold values from -6 to 6
- draft_values: bfloat16 [8, 64, 256], P('dp', 'tok', 'head'), may hold values from -6 to 6
- cached_key_rows: bfloat16 [8, 4096, 256], P('dp', 'tok', 'head'), may hold values from -4 to 4
- cache_values: bfloat16 [8, 4096, 256], P('dp', 'tok', 'head'), may hold values from -6 to 6
- cache_len: int32 [8], P('dp'), may hold values from 2 to 4096
- accepted: int32 [8], P('dp'), may hold values from 0 to 64
Outputs:
- mamba_out: bfloat16 [64, 8, 4096], P(('head', 'tok'), 'dp')
- attn_context: bfloat16 [8, 64, 1024], P('dp', 'tok', 'head')
- committed_state: bfloat16 [8, 32, 64, 128], P('dp', 'head', None, 'tok')
Inputs may be any that keep to these rules, and one draw needn't show every extreme that they name: Each sequence's cached positions 0 to cache_len - 1 are valid.
All inputs are finite; a program needn't handle non-finite values.
Results may differ from a plain program's by a relative error of at most 0.018.
Values may be sent and summed in bfloat16 or wider, within the bound.
A program may use at most 64 MiB of HBM per device.

v0:
```python
import jax
import jax.numpy as jnp
from jax import lax
from jax.sharding import PartitionSpec as P

PRECISE = lax.Precision.HIGHEST
EPSILON = 1e-05
MASKED = -1e30


def within_block(running, step_sizes, feature_values, inflow, readout):
    count = running.shape[1]
    position = jnp.arange(count)
    causal = (position[:, None] >= position[None, :])[None, :, :, None]
    log_gaps = jnp.where(causal, running[:, :, None, :] - running[:, None, :, :], 0.0)
    decays = jnp.where(causal, jnp.exp(log_gaps), 0.0)
    affinity = jnp.einsum("bsn,brn->bsr", readout, inflow, precision=PRECISE)
    mixing = affinity[..., None] * decays * step_sizes[:, None, :, :]
    return jnp.einsum("bsrh,brhp->bshp", mixing, feature_values, precision=PRECISE)


def select_state(limit, log_decay, running, step_sizes, feature_values, inflow, start_state):
    count = running.shape[1]
    alive = (jnp.arange(count)[None, :] < limit[:, None])[..., None]
    end_log = jnp.sum(jnp.where(alive, log_decay, 0.0), axis=1)
    weights = jnp.where(
        alive, jnp.exp(jnp.where(alive, end_log[:, None, :] - running, 0.0)) * step_sizes, 0.0
    )
    return jnp.exp(end_log)[..., None, None] * start_state + jnp.einsum(
        "brh,brhp,brn->bhpn", weights, feature_values, inflow, precision=PRECISE
    )


def body(
    mamba_input,
    gate_input,
    in_b,
    in_c,
    step_size,
    decay_rate,
    skip_weight,
    norm_gain,
    ssm_state,
    out_weight,
    queries,
    draft_token_keys,
    draft_values,
    cached_key_rows,
    cache_values,
    cache_len,
    accepted,
):
    sequences, block_len, feature_width = mamba_input.shape
    head_count = decay_rate.shape[0]
    head_size = feature_width // head_count
    tok_count = lax.axis_size("tok")
    tok_index = lax.axis_index("tok")
    first_draft = tok_index * block_len
    feature_values = mamba_input.astype(jnp.float32).reshape(
        sequences, block_len, head_count, head_size
    )
    inflow_cols, readout_cols = (
        lax.all_to_all(in_b, "tok", split_axis=2, concat_axis=1, tiled=True),
        lax.all_to_all(in_c, "tok", split_axis=2, concat_axis=1, tiled=True),
    )
    all_inputs, all_steps = (
        lax.all_gather(mamba_input, "tok", axis=1, tiled=True),
        lax.all_gather(step_size, "tok", axis=1, tiled=True),
    )
    draft_len = all_inputs.shape[1]
    all_features = all_inputs.astype(jnp.float32).reshape(
        sequences, draft_len, head_count, head_size
    )
    step_sizes = all_steps.astype(jnp.float32)
    inflow = inflow_cols.astype(jnp.float32)
    readout = readout_cols.astype(jnp.float32)
    log_decay = -step_sizes * decay_rate[None, None, :]
    running = jnp.cumsum(log_decay, axis=1)
    within = within_block(running, step_sizes, all_features, inflow, readout)
    start_state = ssm_state.astype(jnp.float32)
    carried = (
        jnp.einsum("bsn,bhpn->bshp", readout, start_state, precision=PRECISE)
        * jnp.exp(running)[..., None]
    )
    partial_sum = (within + carried).reshape(sequences, draft_len, feature_width)
    mixed = (
        lax.psum_scatter(partial_sum.astype(jnp.bfloat16), "tok", scatter_dimension=1, tiled=True)
        .astype(jnp.float32)
        .reshape(sequences, block_len, head_count, head_size)
    )
    chosen = select_state(
        accepted, log_decay, running, step_sizes, all_features, inflow, start_state
    )
    committed_state = chosen.astype(jnp.bfloat16)
    mixed = mixed + skip_weight[None, None, :, None] * feature_values
    gated = mixed.reshape(sequences, block_len, feature_width) * jax.nn.silu(
        gate_input.astype(jnp.float32)
    )
    mean_sq = jnp.mean(gated * gated, axis=-1, keepdims=True)
    normed = (gated * lax.rsqrt(mean_sq + EPSILON) * norm_gain).astype(jnp.bfloat16)
    regrouped = lax.all_to_all(normed, "tok", split_axis=2, concat_axis=1, tiled=True)
    mamba_out = lax.psum_scatter(
        jnp.einsum("sdf,fo->dso", regrouped, out_weight, preferred_element_type=jnp.float32).astype(
            jnp.bfloat16
        ),
        ("head", "tok"),
        scatter_dimension=0,
        tiled=True,
    )
    all_queries = lax.all_gather(queries, "tok", axis=1, tiled=True)
    att_size = draft_token_keys.shape[2]
    per_kv = queries.shape[2] // att_size
    draft_len = all_queries.shape[1]
    cache_block = cached_key_rows.shape[1]
    query_matrix = all_queries.reshape(sequences, draft_len * per_kv, att_size)
    score_scale = att_size ** (-0.5)
    cache_scores = (
        jnp.einsum(
            "cmq,czq->cmz", query_matrix, cached_key_rows, preferred_element_type=jnp.float32
        )
        * score_scale
    )
    draft_scores = (
        jnp.einsum(
            "cmq,czq->cmz", query_matrix, draft_token_keys, preferred_element_type=jnp.float32
        )
        * score_scale
    )
    cache_pos = tok_index * cache_block + jnp.arange(cache_block)
    cache_valid = cache_pos[None, None, :] < cache_len[:, None, None]
    query_pos = jnp.repeat(jnp.arange(draft_len), per_kv)
    draft_valid = ((first_draft + jnp.arange(block_len))[None, :] <= query_pos[:, None])[None, :, :]
    cache_scores = jnp.where(cache_valid, cache_scores, MASKED)
    draft_scores = jnp.where(draft_valid, draft_scores, MASKED)
    row_peak = jnp.maximum(jnp.max(cache_scores, axis=-1), jnp.max(draft_scores, axis=-1))
    cache_probs = jnp.where(cache_valid, jnp.exp(cache_scores - row_peak[..., None]), 0.0)
    draft_probs = jnp.where(draft_valid, jnp.exp(draft_scores - row_peak[..., None]), 0.0)
    row_total = jnp.sum(cache_probs, axis=-1) + jnp.sum(draft_probs, axis=-1)
    numer = jnp.einsum(
        "ces,csx->cex",
        cache_probs.astype(jnp.bfloat16),
        cache_values,
        preferred_element_type=jnp.float32,
    )
    numer = numer + jnp.einsum(
        "ces,csx->cex",
        draft_probs.astype(jnp.bfloat16),
        draft_values,
        preferred_element_type=jnp.float32,
    )
    peaks, totals, numers = (
        lax.all_to_all(
            row_peak.reshape(1, sequences, draft_len, per_kv).astype(jnp.bfloat16),
            "tok",
            split_axis=2,
            concat_axis=0,
            tiled=True,
        ).astype(jnp.float32),
        lax.all_to_all(
            row_total.reshape(1, sequences, draft_len, per_kv).astype(jnp.bfloat16),
            "tok",
            split_axis=2,
            concat_axis=0,
            tiled=True,
        ).astype(jnp.float32),
        lax.all_to_all(
            numer.reshape(1, sequences, draft_len, per_kv * att_size).astype(jnp.bfloat16),
            "tok",
            split_axis=2,
            concat_axis=0,
            tiled=True,
        ).astype(jnp.float32),
    )
    overall = jnp.max(peaks, axis=0)
    rescale = jnp.exp(peaks - overall[None])
    denominator = jnp.sum(rescale * totals, axis=0)
    numers = numers.reshape(tok_count, sequences, block_len, per_kv, att_size)
    context = jnp.sum(rescale[..., None] * numers, axis=0) / denominator[..., None]
    attn_context = context.reshape(sequences, block_len, per_kv * att_size).astype(jnp.bfloat16)
    return (mamba_out, attn_context, committed_state)


def solution(mesh):
    in_specs = (
        P("dp", "tok", "head"),
        P("dp", "tok", "head"),
        P("dp", "tok", "head"),
        P("dp", "tok", "head"),
        P("dp", "tok", "head"),
        P("head"),
        P("head"),
        P("head"),
        P("dp", "head", None, "tok"),
        P(("head", "tok"), None),
        P("dp", "tok", "head"),
        P("dp", "tok", "head"),
        P("dp", "tok", "head"),
        P("dp", "tok", "head"),
        P("dp", "tok", "head"),
        P("dp"),
        P("dp"),
    )
    out_specs = (
        P(("head", "tok"), "dp", None),
        P("dp", "tok", "head"),
        P("dp", "head", None, "tok"),
    )
    return jax.shard_map(body, mesh=mesh, in_specs=in_specs, out_specs=out_specs, check_vma=False)
```

profile of v0, /device:TPU:0, one launch (start us, length us, event | category | flops | bytes accessed | tf_op | source)
XLA Modules:
  0.0 129.2 jit_solution(7168623437483641221)
XLA Ops:
  7.2 1.0 copy.64
  8.2 0.7 reshape.252
  8.9 4.4 %all-to-all-start = ((bf16[4,2,512]{2,1,0:T(2,128)(2,1)}), bf16[4,2,512]{2,1,0:T(2,128)(2,1)S(1)}, u32[]{:S(2)}, u32[]{:S(2)}) async-start(bf16[4,2,512]{2,1,0:T(2,128)(2,1)} %reshape.252), calls=%async_computation | async-start | bytes 16384 | tf_op jit(solution)/shard_map/all_to_all | solution.py:64
  13.3 5.8 %all_gather.11 = bf16[2,64,512]{2,1,0:T(8,128)(2,1)S(1)} all-gather(bf16[2,16,512]{2,1,0:T(8,128)(2,1)} %param.27), channel_id=1, replica_groups=mesh['dp'=4,'head'=2,'tok'=4] {'tok'}, dimensions={1}, use_global_device_ids=true | all-gather | bytes 163840 | tf_op jit(solution)/shard_map/all_gather | solution.py:110
  19.0 0.1 reshape.243
  19.2 0.1 le.20
  19.3 5.6 %all_gather.9 = bf16[2,64,16]{2,1,0:T(8,128)(2,1)S(1)} all-gather(bf16[2,16,16]{2,1,0:T(8,128)(2,1)} %param.21), channel_id=1, replica_groups=mesh['dp'=4,'head'=2,'tok'=4] {'tok'}, dimensions={1}, use_global_device_ids=true | all-gather | bytes 5120 | tf_op jit(solution)/shard_map/all_gather | solution.py:68
  24.8 0.7 iota_compare_fusion.1
  25.6 0.7 broadcast_compare_fusion.1
  26.4 2.8 %fusion.2 = (f32[2,256]{1,0:T(2,128)S(1)}, f32[2,256,1024]{2,1,0:T(8,128)}) fusion(pred[2,1024]{1,0:T(4,128)(4,1)S(1)} %broadcast_compare_fusion.1, bf16[2,256,128]{2,1,0:T(8,128)(2,1)S(1)} %reshape.243, bf16[2,1024,128]{2,1,0:T(8,128)(2,1)} %param.30), kind=kOutput, calls=%fused_computation.5 | convolution fusion | flops 135790080 | bytes 2756608 | tf_op jit(solution)/shard_map/cmq,czq->cmz/dot_general | solution.py:118
  29.2 0.2 fusion.56
  29.4 0.1 select_reduce_fusion
  29.5 0.1 reduce_window_sum.11
  29.6 0.1 multiply_select_fusion.1
  29.7 0.1 copy.66
  29.8 0.7 reshape.254
  30.6 3.2 %all-to-all-start.1 = ((bf16[4,2,512]{2,1,0:T(2,128)(2,1)}), bf16[4,2,512]{2,1,0:T(2,128)(2,1)S(1)}, u32[]{:S(2)}, u32[]{:S(2)}) async-start(bf16[4,2,512]{2,1,0:T(2,128)(2,1)} %reshape.254), calls=%async_computation.1 | async-start | bytes 16384 | tf_op jit(solution)/shard_map/all_to_all | solution.py:63
  33.9 6.2 %all_gather.10 = bf16[2,64,1024]{2,1,0:T(8,128)(2,1)S(1)} all-gather(bf16[2,16,1024]{2,1,0:T(8,128)(2,1)S(1)} %copy-done.3), channel_id=1, replica_groups=mesh['dp'=4,'head'=2,'tok'=4] {'tok'}, dimensions={1}, use_global_device_ids=true | all-gather | bytes 327680 | tf_op jit(solution)/shard_map/all_gather | solution.py:67
  40.2 0.1 copy.75
  40.3 0.3 reshape.242
  40.6 0.1 reshape.253
  40.7 0.1 copy.65
  40.8 0.1 reshape.255
  41.0 0.1 copy.67
  41.1 0.1 fusion.57
  41.2 1.0 convolution_bitcast_fusion
  42.2 0.4 fusion.6
  42.6 0.3 copy.76
  43.0 1.1 convert_element_type.122
  44.2 1.0 fusion.44
  45.2 2.2 %fusion.3 = f32[2,256]{1,0:T(2,128)S(1)} fusion(f32[2,256,1024]{2,1,0:T(8,128)} %get-tuple-element.26, f32[2,256]{1,0:T(2,128)S(1)} %get-tuple-element.16, pred[2,1024]{1,0:T(4,128)(4,1)S(1)} %broadcast_compare_fusion.1), kind=kLoop, calls=%fused_computation.6 | loop fusion | flops 2620928 | bytes 2103296 | tf_op jit(solution)/shard_map/reduce_sum | solution.py:138
  47.4 18.6 %reduce-scatter.5.cloned.1.call-done = bf16[2,16,1024]{2,1,0:T(8,128)(2,1)} async-done(((bf16[2,64,1024]{2,1,0:T(8,128)(2,1)}), bf16[2,16,1024]{2,1,0:T(8,128)(2,1)}) %reduce-scatter.5.cloned.1.call-update) | async-done | bytes 65552 | tf_op jit(solution)/shard_map/reduce_scatter | solution.py:87
  66.0 1.0 multiply_reduce_fusion
  67.0 0.1 multiply_convert_fusion
  67.1 0.4 copy.77
  67.5 1.2 reshape.256
  68.7 3.3 %all-to-all-start.2 = ((bf16[4,2,4096]{2,1,0:T(2,128)(2,1)}), bf16[4,2,4096]{2,1,0:T(2,128)(2,1)S(1)}, u32[]{:S(2)}, u32[]{:S(2)}) async-start(bf16[4,2,4096]{2,1,0:T(2,128)(2,1)} %reshape.256), calls=%async_computation.3 | async-start | bytes 131072 | tf_op jit(solution)/shard_map/all_to_all | solution.py:101
  72.0 0.1 convert_element_type.130
  72.1 0.7 copy.79
  72.8 3.3 %all-to-all-done.2 = bf16[4,2,4096]{2,1,0:T(2,128)(2,1)S(1)} async-done(((bf16[4,2,4096]{2,1,0:T(2,128)(2,1)}), bf16[4,2,4096]{2,1,0:T(2,128)(2,1)S(1)}, u32[]{:S(2)}, u32[]{:S(2)}) %all-to-all-start.2) | async-done | bytes 65568 | tf_op jit(solution)/shard_map/all_to_all | solution.py:101
  76.0 3.3 %all-to-all-start.3 = ((bf16[1,2,64,4]{3,1,0,2:T(2,128)(2,1)}), bf16[1,2,64,4]{3,1,0,2:T(2,128)(2,1)S(1)}, u32[]{:S(2)}, u32[]{:S(2)}) async-start(bf16[1,2,64,4]{3,1,0,2:T(2,128)(2,1)} %copy.79), calls=%async_computation.4 | async-start | bytes 65536 | tf_op jit(solution)/shard_map/all_to_all | solution.py:152
  79.4 0.4 reshape.257
  79.8 0.3 copy.78
  80.1 0.4 fusion
  80.6 1.1 copy.94
  81.7 0.1 convert_element_type.141
  81.8 0.7 copy.81
  82.4 0.8 all-to-all-done.3
  83.2 3.3 %all-to-all-start.5 = ((bf16[1,2,64,4]{3,1,0,2:T(2,128)(2,1)}), bf16[1,2,64,4]{3,1,0,2:T(2,128)(2,1)S(1)}, u32[]{:S(2)}, u32[]{:S(2)}) async-start(bf16[1,2,64,4]{3,1,0,2:T(2,128)(2,1)} %copy.81), calls=%async_computation.6 | async-start | bytes 65536 | tf_op jit(solution)/shard_map/all_to_all | solution.py:159
  86.5 2.3 %fusion.9 = bf16[2,256,128]{2,1,0:T(8,128)(2,1)S(1)} fusion(f32[2,256,128]{2,1,0:T(8,128)S(1)} %copy-done.2, bf16[2,1024,128]{2,1,0:T(8,128)(2,1)} %param.31, f32[2,256,1024]{2,1,0:T(8,128)} %get-tuple-element.26, f32[2,256]{1,0:T(2,128)S(1)} %get-tuple-element.16, pred[2,1024]{1,0:T(4,128)(4,1)S(1)} %broadcast_compare_fusion.1), kind=kOutput, calls=%fused_computation.16 | convolution fusion | flops 136970240 | bytes 3018752 | tf_op jit(solution)/shard_map/ces,csx->cex/dot_general | solution.py:139
  88.9 0.1 convert_element_type.136
  89.0 0.8 copy.80
  89.9 0.5 all-to-all-done.5
  90.4 3.3 %all-to-all-start.4 = ((bf16[1,2,64,512]{3,1,0,2:T(2,128)(2,1)}), bf16[1,2,64,512]{3,1,0,2:T(2,128)(2,1)S(1)}, u32[]{:S(2)}, u32[]{:S(2)}) async-start(bf16[1,2,64,512]{3,1,0,2:T(2,128)(2,1)} %copy.80), calls=%async_computation.5 | async-start | bytes 262144 | tf_op jit(solution)/shard_map/all_to_all | solution.py:166
  93.8 0.1 fusion.40
  93.8 0.2 mul.139
  94.0 0.2 mul.140
  94.3 0.1 div.24
  94.5 2.3 %fusion.8 = bf16[2,16,64,32]{2,3,1,0:T(8,128)(2,1)} fusion(bf16[2,16,64,32]{2,3,1,0:T(8,128)(2,1)} %param.25, bf16[2,64,16,64]{3,2,1,0:T(8,128)(2,1)S(1)} %reshape.242, f32[2,64,32]{1,2,0:T(8,128)S(1)} %copy.83, f32[2,64,16]{1,2,0:T(8,128)S(1)} %copy.82, f32[2,16]{1,0:T(2,128)S(1)} %exp.43), kind=kOutput, calls=%fused_computation.14 | convolution fusion | flops 50659328 | bytes 548992 | tf_op jit(solution)/shard_map/brh,brhp,brn->bhpn/dot_general | solution.py:29
  96.8 1.6 %all-to-all-done.4 = bf16[1,2,64,512]{3,1,0,2:T(2,128)(2,1)S(1)} async-done(((bf16[1,2,64,512]{3,1,0,2:T(2,128)(2,1)}), bf16[1,2,64,512]{3,1,0,2:T(2,128)(2,1)S(1)}, u32[]{:S(2)}, u32[]{:S(2)}) %all-to-all-start.4) | async-done | bytes 131104 | tf_op jit(solution)/shard_map/all_to_all | solution.py:166
  98.3 0.2 fusion.33
  98.5 0.6 copy.86
  99.1 21.6 %reduce-scatter.7.cloned.1.call-done = bf16[8,8192]{1,0:T(8,128)(2,1)} async-done(((bf16[64,8192]{1,0:T(8,128)(2,1)}), bf16[8,8192]{1,0:T(8,128)(2,1)}) %reduce-scatter.7.cloned.1.call-update) | async-done | bytes 131088
  120.7 1.7 %copy.85 = bf16[8,2,4096]{2,1,0:T(2,128)(2,1)} copy(bf16[8,2,4096]{2,0,1:T(8,128)(2,1)} %bitcast.97) | data formatting | bytes 262144
  (49 shorter events, 0.9 us)
Async XLA Ops:
  7.2 72.9 %copy-start = (bf16[256,4096]{1,0:T(8,128)(2,1)S(1)}, bf16[256,4096]{1,0:T(8,128)(2,1)}, u32[]{:S(2)}) copy-start(bf16[256,4096]{1,0:T(8,128)(2,1)} %param.26) | copy-start | bytes 6291460
  7.2 22.0 %copy-start.5 = (bf16[2,16,128]{2,1,0:T(8,128)(2,1)S(1)}, bf16[2,16,128]{2,1,0:T(8,128)(2,1)}, u32[]{:S(2)}) copy-start(bf16[2,16,128]{2,1,0:T(8,128)(2,1)} %param.28) | copy-start | bytes 24580
  7.2 22.2 %copy-start.9 = (f32[16]{0:T(128)S(1)}, f32[16]{0:T(128)}, u32[]{:S(2)}) copy-start(f32[16]{0:T(128)} %param.22) | copy-start | bytes 196
  7.2 22.5 %copy-start.6 = (bf16[2,16,128]{2,1,0:T(8,128)(2,1)S(1)}, bf16[2,16,128]{2,1,0:T(8,128)(2,1)}, u32[]{:S(2)}) copy-start(bf16[2,16,128]{2,1,0:T(8,128)(2,1)} %param.19) | copy-start | bytes 24580
  8.9 25.0 %copy-start.3 = (bf16[2,16,1024]{2,1,0:T(8,128)(2,1)S(1)}, bf16[2,16,1024]{2,1,0:T(8,128)(2,1)}, u32[]{:S(2)}) copy-start(bf16[2,16,1024]{2,1,0:T(8,128)(2,1)} %param.17) | copy-start | bytes 196612
  8.9 21.7 %all-to-all-start = ((bf16[4,2,512]{2,1,0:T(2,128)(2,1)}), bf16[4,2,512]{2,1,0:T(2,128)(2,1)S(1)}, u32[]{:S(2)}, u32[]{:S(2)}) async-start(bf16[4,2,512]{2,1,0:T(2,128)(2,1)} %reshape.252), calls=%async_computation | async-start | bytes 16384 | tf_op jit(solution)/shard_map/all_to_all | solution.py:64
  30.6 10.3 %all-to-all-start.1 = ((bf16[4,2,512]{2,1,0:T(2,128)(2,1)}), bf16[4,2,512]{2,1,0:T(2,128)(2,1)S(1)}, u32[]{:S(2)}, u32[]{:S(2)}) async-start(bf16[4,2,512]{2,1,0:T(2,128)(2,1)} %reshape.254), calls=%async_computation.1 | async-start | bytes 16384 | tf_op jit(solution)/shard_map/all_to_all | solution.py:63
  33.8 32.2 %reduce-scatter.5.cloned.1.call-start = ((), (), s32[]{:S(2)}) async-start(), calls=%async_computation.8 | async-start | bytes 327680 | tf_op jit(solution)/shard_map/reduce_scatter | solution.py:87
  40.1 2.1 %copy-start.1 = (bf16[2,16,64,32]{2,3,1,0:T(8,128)(2,1)S(1)}, bf16[2,16,64,32]{2,3,1,0:T(8,128)(2,1)}, u32[]{:S(2)}) copy-start(bf16[2,16,64,32]{2,3,1,0:T(8,128)(2,1)} %param.25) | copy-start | bytes 393220
  42.2 1.9 %copy-start.10 = (f32[16]{0:T(128)S(1)}, f32[16]{0:T(128)}, u32[]{:S(2)}) copy-start(f32[16]{0:T(128)} %param.23) | copy-start | bytes 196
  42.2 2.0 %copy-start.7 = (bf16[2,16,128]{2,1,0:T(8,128)(2,1)S(1)}, bf16[2,16,128]{2,1,0:T(8,128)(2,1)}, u32[]{:S(2)}) copy-start(bf16[2,16,128]{2,1,0:T(8,128)(2,1)} %param.29) | copy-start | bytes 24580
  42.6 23.4 %copy-start.4 = (bf16[2,16,1024]{2,1,0:T(8,128)(2,1)S(1)}, bf16[2,16,1024]{2,1,0:T(8,128)(2,1)}, u32[]{:S(2)}) copy-start(bf16[2,16,1024]{2,1,0:T(8,128)(2,1)} %param.18) | copy-start | bytes 196612
  43.0 24.0 %copy-start.8 = (f32[1024]{0:T(1024)S(1)}, f32[1024]{0:T(1024)}, u32[]{:S(2)}) copy-start(f32[1024]{0:T(1024)} %param.24) | copy-start | bytes 12292
  68.7 7.4 %all-to-all-start.2 = ((bf16[4,2,4096]{2,1,0:T(2,128)(2,1)}), bf16[4,2,4096]{2,1,0:T(2,128)(2,1)S(1)}, u32[]{:S(2)}, u32[]{:S(2)}) async-start(bf16[4,2,4096]{2,1,0:T(2,128)(2,1)} %reshape.256), calls=%async_computation.3 | async-start | bytes 131072 | tf_op jit(solution)/shard_map/all_to_all | solution.py:101
  76.0 7.2 %all-to-all-start.3 = ((bf16[1,2,64,4]{3,1,0,2:T(2,128)(2,1)}), bf16[1,2,64,4]{3,1,0,2:T(2,128)(2,1)S(1)}, u32[]{:S(2)}, u32[]{:S(2)}) async-start(bf16[1,2,64,4]{3,1,0,2:T(2,128)(2,1)} %copy.79), calls=%async_computation.4 | async-start | bytes 65536 | tf_op jit(solution)/shard_map/all_to_all | solution.py:152
  79.3 41.4 %reduce-scatter.7.cloned.1.call-start = ((), (), s32[]{:S(2)}) async-start(), calls=%async_computation.9 | async-start | bytes 1179648
  80.5 6.0 %copy-start.2 = (f32[2,256,128]{2,1,0:T(8,128)S(1)}, f32[2,256,128]{2,1,0:T(8,128)}, u32[]{:S(2)}) copy-start(f32[2,256,128]{2,1,0:T(8,128)} %fusion.44) | copy-start | bytes 786436
  83.2 7.2 %all-to-all-start.5 = ((bf16[1,2,64,4]{3,1,0,2:T(2,128)(2,1)}), bf16[1,2,64,4]{3,1,0,2:T(2,128)(2,1)S(1)}, u32[]{:S(2)}, u32[]{:S(2)}) async-start(bf16[1,2,64,4]{3,1,0,2:T(2,128)(2,1)} %copy.81), calls=%async_computation.6 | async-start | bytes 65536 | tf_op jit(solution)/shard_map/all_to_all | solution.py:159
  90.4 7.9 %all-to-all-start.4 = ((bf16[1,2,64,512]{3,1,0,2:T(2,128)(2,1)}), bf16[1,2,64,512]{3,1,0,2:T(2,128)(2,1)S(1)}, u32[]{:S(2)}, u32[]{:S(2)}) async-start(bf16[1,2,64,512]{3,1,0,2:T(2,128)(2,1)} %copy.80), calls=%async_computation.5 | async-start | bytes 262144 | tf_op jit(solution)/shard_map/all_to_all | solution.py:166
Sparse Core Ops, SparseCore 0:
  44.2 21.7 reduce-scatter.4
  83.3 37.3 reduce-scatter.6
where the time goes:
time: 130 us; the launch traced here: 129 us
  waiting for transfers between devices  46.4 us (36%)
  starting transfers between devices  20.8 us (16%)
  blocking collectives  17.5 us (13%)
  between operations  14.5 us (11%)
  local copies, waits for them, and re-layouts  14 us (11%)
  matrix products  10.5 us (8%)
  other arithmetic  5.51 us (4%)
    unnamed x3, waiting for transfers between devices  21.6 us
    reduce_scatter x1, waiting for transfers between devices, body(): lax.psum_scatter(partial_sum.astype(jnp.bfloat16), 'tok', scatter_dimensi...  18.6 us
    unnamed x33, local copies, waits for them, and re-layouts  7.74 us
    all_gather x1, blocking collectives, body(): lax.all_gather(mamba_input, 'tok', axis=1, tiled=True)  6.17 us
    all_gather x1, blocking collectives, body(): all_queries = lax.all_gather(queries, 'tok', axis=1, tiled=True)  5.76 us
    all_gather x1, blocking collectives, body(): lax.all_gather(step_size, 'tok', axis=1, tiled=True)  5.57 us
    all_to_all x1, starting transfers between devices, body(): lax.all_to_all(in_c, 'tok', split_axis=2, concat_axis=1, tiled=True)  4.37 us
    all_to_all x1, starting transfers between devices, body(): lax.all_to_all(numer.reshape(1, sequences, draft_len, per_kv * att_size)....  3.33 us
  transfers between devices with their start and end apart: 8, of which 6 were waited for; matrix products, arithmetic and copies ran while one was open for 16% of the time, Pallas kernels for 0%

commit v1 on v0

v1 whole, which is shorter than its diff:
```python
import functools
import jax
import jax.numpy as jnp
from jax import lax
from jax.experimental import pallas as pl
from jax.experimental.pallas import tpu as pltpu
from jax.sharding import PartitionSpec as P

EPSILON = 1e-05
MASKED = -1e30
FLOOR = -1e29
MESH = pl.DeviceIdType.MESH
F32 = jnp.float32
BF16 = jnp.bfloat16
NT = (((1,), (1,)), ((), ()))


def dot(a, b):
    return jnp.dot(a, b, preferred_element_type=F32)


def iota(shape, dim):
    return lax.broadcasted_iota(jnp.int32, shape, dim)


def kernel(
    dims,
    x_in, z_in, b_in, c_in, dt_in, st_in, q_in, k_in, v_in, w_in,
    dk_ref, dv_ref, gain_ref, rate_ref, skip_ref, len_ref, acc_ref,
    out_ref, ctx_ref, com_ref,
    x_l, z_l, b_l, c_l, dt_l, st_l, q_l, k_v, v_v, w_v,
    ss_l, cm_s, cm_l, n_s, n_l, stat_l, part, rs_l,
    send, recv, rs_send, rs_recv, local,
):
    n_head, n_tok, seqs, block, heads, chunks = dims
    group = n_head * n_tok
    tok = lax.axis_index("tok")
    head = lax.axis_index("head")
    me = head * n_tok + tok
    draft = block * n_tok
    width = x_l.shape[2]
    own = heads // n_tok
    size = width // own
    state = st_l.shape[1]
    cols = state // n_tok
    att = k_v.shape[2]
    per_kv = q_l.shape[2] // att
    cache = k_v.shape[1]
    rows = seqs * draft
    each = rows // group
    out_cols = w_v.shape[1]
    span = out_cols // chunks

    def place(index, unit):
        return pl.ds(pl.multiple_of(index * unit, unit), unit)

    barrier = pltpu.get_barrier_semaphore()
    for o in range(1, group):
        peer = lax.rem(me + o, group)
        pl.semaphore_signal(
            barrier, inc=1,
            device_id={"head": peer // n_tok, "tok": lax.rem(peer, n_tok)},
            device_id_type=MESH,
        )

    mine = place(tok, block)
    locals_ = [
        (x_in.at[:, :, place(tok, width)], x_l.at[:, mine, :]),
        (z_in.at[:, :, place(tok, width)], z_l.at[:, mine, :]),
        (b_in, b_l.at[:, mine, :]),
        (c_in, c_l.at[:, mine, :]),
        (dt_in, dt_l.at[:, mine, :]),
        (st_in.at[:, :, place(tok, width)], st_l.at[:, place(tok, cols), :]),
        (q_in, q_l.at[:, mine, :]),
        (w_in, w_v),
        (k_in, k_v),
        (v_in, v_v),
    ]
    held = [
        pltpu.make_async_copy(src, dst, local.at[i]) for i, (src, dst) in enumerate(locals_)
    ]
    for copy in held:
        copy.start()

    pl.semaphore_wait(barrier, group - 1)

    def remote(kind, o, src, dst):
        return pltpu.make_async_remote_copy(
            src_ref=src, dst_ref=dst,
            send_sem=send.at[kind, o], recv_sem=recv.at[kind, o],
            device_id={"tok": lax.rem(tok + o, n_tok)}, device_id_type=MESH,
        )

    started = []

    def ship(kind, o, src, dst):
        copy = remote(kind, o, src, dst)
        copy.start()
        started.append(copy)

    first = {}
    for o in range(1, n_tok):
        to = lax.rem(tok + o, n_tok)
        pairs = [
            (dt_in, dt_l.at[:, mine, :]),
            (b_in, b_l.at[:, mine, :]),
            (c_in, c_l.at[:, mine, :]),
            (x_in.at[:, :, place(to, width)], x_l.at[:, mine, :]),
            (st_in.at[:, :, place(to, width)], st_l.at[:, place(tok, cols), :]),
            (z_in.at[:, :, place(to, width)], z_l.at[:, mine, :]),
        ]
        for kind, (src, dst) in enumerate(pairs):
            ship(kind, o, src, dst)
            first[kind, o] = started[-1]
    for o in range(1, n_tok):
        ship(6, o, q_in, q_l.at[:, mine, :])
        first[6, o] = started[-1]

    for copy in held[:6]:
        copy.wait()
    for kind in range(6):
        for o in range(1, n_tok):
            first[kind, o].wait_recv()

    lane = iota((1, width), 1)
    rate_x = jnp.zeros((1, width), F32)
    skip_x = jnp.zeros((1, width), F32)
    for h in range(own):
        inside = (lane >= h * size) & (lane < (h + 1) * size)
        rate_x = jnp.where(inside, rate_ref[tok * own + h], rate_x)
        skip_x = jnp.where(inside, skip_ref[tok * own + h], skip_x)
    offset = iota((heads, width), 1) - (iota((heads, width), 0) - tok * own) * size
    pick = ((offset >= 0) & (offset < size)).astype(F32).astype(BF16)
    causal = iota((draft, draft), 0) >= iota((draft, draft), 1)
    lower = causal.astype(F32).astype(BF16)

    gated = []
    saved = []
    for s in range(seqs):
        x = x_l[s].astype(F32)
        z = z_l[s].astype(F32)
        b = b_l[s]
        c = c_l[s]
        st = st_l[s]
        dtx = dot(dt_l[s], pick)
        run = -rate_x * dot(lower, dtx.astype(BF16))
        scaled = (x * dtx * jnp.exp(-run)).astype(BF16)
        mix = lax.dot_general(c, b, NT, preferred_element_type=F32)
        mix = jnp.where(causal, mix, 0.0).astype(BF16)
        y = jnp.exp(run) * (dot(mix, scaled) + dot(c, st)) + skip_x * x
        gated.append(y * z / (1.0 + jnp.exp(-z)))
        saved.append((x, dtx, run))
    gated = jnp.concatenate(gated, axis=0)
    sums = jnp.sum(gated * gated, axis=1, keepdims=True)
    eye = iota((rows, rows), 0) == iota((rows, rows), 1)
    sum_row = jnp.sum(jnp.where(eye, sums, 0.0), axis=0, keepdims=True)
    ss_l[tok] = jnp.broadcast_to(sum_row, (8, rows))
    for o in range(1, n_tok):
        ship(7, o, ss_l.at[tok], ss_l.at[tok])
        first[7, o] = started[-1]

    for s in range(seqs):
        x, dtx, run = saved[s]
        alive = iota((draft, width), 0) < acc_ref[s]
        end = -rate_x * jnp.sum(jnp.where(alive, dtx, 0.0), axis=0, keepdims=True)
        weight = jnp.where(alive, jnp.exp(jnp.where(alive, end - run, 0.0)) * dtx, 0.0)
        flow = b_l[s].astype(F32).T.astype(BF16)
        new = jnp.exp(end) * st_l[s].astype(F32) + dot(flow, (x * weight).astype(BF16))
        cm_s[s] = new.astype(BF16)

    for o in range(1, n_tok):
        first[7, o].wait_recv()
    totals = jnp.zeros((1, rows), F32)
    for t in range(n_tok):
        totals = totals + ss_l[t][0:1, :]
    col = jnp.sum(jnp.where(eye, totals, 0.0), axis=1, keepdims=True)
    gain = gain_ref[:, place(tok, width)]
    normed = gated * lax.rsqrt(col / (width * n_tok) + EPSILON) * gain
    swap = None
    for s in range(seqs):
        k = iota((rows, rows), 1) - s * draft
        hit = (k >= 0) & (k < draft) & (k * seqs + s == iota((rows, rows), 0))
        swap = hit if swap is None else swap | hit
    normed = dot(swap.astype(F32).astype(BF16), normed.astype(BF16)).astype(BF16)

    held[7].wait()
    tile = min(512, span)
    rs = {}
    for ch in range(chunks):
        for start in range(ch * span, (ch + 1) * span, tile):
            val = dot(normed, w_v[:, start : start + tile]).astype(BF16)
            for g in range(group):
                part[g, :, start : start + tile] = val[g * each : (g + 1) * each]
        for o in range(1, group):
            peer = lax.rem(me + o, group)
            piece = pl.ds(ch * span, span)
            copy = pltpu.make_async_remote_copy(
                src_ref=part.at[peer, :, piece], dst_ref=rs_l.at[o, :, piece],
                send_sem=rs_send.at[ch, o], recv_sem=rs_recv.at[ch, o],
                device_id={"head": peer // n_tok, "tok": lax.rem(peer, n_tok)},
                device_id_type=MESH,
            )
            copy.start()
            rs[ch, o] = copy

    for o in range(1, n_tok):
        first[6, o].wait_recv()
    held[6].wait()
    held[8].wait()
    held[9].wait()
    scale = att ** (-0.5)
    m_rows = per_kv * draft
    big = iota((m_rows, m_rows), 0) == iota((m_rows, m_rows), 1)
    position = tok * cache + iota((1, cache), 1)
    draft_at = tok * block + iota((draft, block), 1)
    seen = draft_at <= iota((draft, block), 0)
    seen = jnp.concatenate([seen.astype(F32)] * per_kv, axis=0) > 0.5
    for s in range(seqs):
        q = jnp.concatenate([q_l[s, :, h * att : (h + 1) * att] for h in range(per_kv)], axis=0)
        old = lax.dot_general(q, k_v[s], NT, preferred_element_type=F32)
        old = jnp.where(position < len_ref[s], old, MASKED)
        new = lax.dot_general(q, dk_ref[s], NT, preferred_element_type=F32)
        new = jnp.where(seen, new, MASKED)
        peak = jnp.maximum(
            jnp.max(old, axis=1, keepdims=True), jnp.max(new, axis=1, keepdims=True)
        )
        peak = jnp.maximum(peak, FLOOR)
        old = jnp.exp((old - peak) * scale)
        new = jnp.exp((new - peak) * scale)
        total = jnp.sum(old, axis=1, keepdims=True) + jnp.sum(new, axis=1, keepdims=True)
        numer = dot(old.astype(BF16), v_v[s]) + dot(new.astype(BF16), dv_ref[s])
        safe = jnp.maximum(total, 1e-30)
        ctx = (numer / safe).astype(BF16)
        level = jnp.where(total > 0.0, peak * scale + jnp.log(safe), MASKED)
        for h in range(per_kv):
            n_s[s, h] = ctx[h * draft : (h + 1) * draft]
        stat_l[tok, s : s + 1, :] = jnp.sum(jnp.where(big, level, 0.0), axis=0, keepdims=True)
    for o in range(1, n_tok):
        to = lax.rem(tok + o, n_tok)
        ship(8, o, stat_l.at[tok], stat_l.at[tok])
        first[8, o] = started[-1]
        ship(9, o, n_s.at[:, :, place(to, block), :], n_l.at[tok])
        first[9, o] = started[-1]
    for o in range(1, n_tok):
        to = lax.rem(tok + o, n_tok)
        ship(10, o, cm_s.at[:, place(to, cols), :], cm_l.at[:, :, place(tok, width)])
        first[10, o] = started[-1]
    n_l[tok] = n_s[:, :, mine, :]
    cm_l[:, :, place(tok, width)] = cm_s[:, place(tok, cols), :]

    for ch in range(chunks):
        for o in range(1, group):
            rs[ch, o].wait_recv()
        for start in range(ch * span, (ch + 1) * span, tile):
            acc = part[me, :, start : start + tile].astype(F32)
            for o in range(1, group):
                acc = acc + rs_l[o, :, start : start + tile].astype(F32)
            out_ref[:, start : start + tile] = acc.astype(BF16)

    for o in range(1, n_tok):
        first[8, o].wait_recv()
        first[9, o].wait_recv()
    m_own = per_kv * block
    lanes = iota((m_own, m_rows), 1)
    r = iota((m_own, m_rows), 0)
    want = None
    for h in range(per_kv):
        t = r - h * block
        hit = (t >= 0) & (t < block) & (lanes == h * draft + tok * block + t)
        want = hit if want is None else want | hit
    for s in range(seqs):
        levels = [
            jnp.sum(jnp.where(want, stat_l[t][s : s + 1, :], 0.0), axis=1, keepdims=True)
            for t in range(n_tok)
        ]
        top = functools.reduce(jnp.maximum, levels)
        weights = [jnp.exp(level - top) for level in levels]
        den = functools.reduce(jnp.add, weights)
        acc = jnp.zeros((m_own, att), F32)
        for t in range(n_tok):
            got = jnp.concatenate([n_l[t, s, h].astype(F32) for h in range(per_kv)], axis=0)
            acc = acc + weights[t] * got
        acc = (acc / den).astype(BF16)
        for h in range(per_kv):
            ctx_ref[s, :, h * att : (h + 1) * att] = acc[h * block : (h + 1) * block]

    for o in range(1, n_tok):
        first[10, o].wait_recv()
    com_ref[...] = cm_l[...]
    for copy in started:
        copy.wait_send()
    for copy in rs.values():
        copy.wait_send()


def body(
    mamba_input, gate_input, in_b, in_c, step_size, decay_rate, skip_weight, norm_gain,
    ssm_state, out_weight, queries, draft_token_keys, draft_values, cached_key_rows,
    cache_values, cache_len, accepted,
):
    n_tok = lax.axis_size("tok")
    n_head = lax.axis_size("head")
    group = n_head * n_tok
    seqs, block, features = mamba_input.shape
    heads = decay_rate.shape[0]
    size = features // heads
    cols = ssm_state.shape[3]
    state = cols * n_tok
    draft = block * n_tok
    width = features // n_tok
    att = draft_token_keys.shape[2]
    per_kv = queries.shape[2] // att
    cache = cached_key_rows.shape[1]
    out_cols = out_weight.shape[1]
    rows = seqs * draft
    each = rows // group
    chunks = 2
    turned = jnp.transpose(ssm_state, (0, 3, 1, 2)).reshape(seqs, cols, features)
    anys = [pl.BlockSpec(memory_space=pl.ANY)] * 10
    vmems = [pl.BlockSpec(memory_space=pltpu.VMEM)] * 3
    smems = [pl.BlockSpec(memory_space=pltpu.SMEM)] * 4
    out, ctx, com = pl.pallas_call(
        functools.partial(kernel, (n_head, n_tok, seqs, block, heads, chunks)),
        out_shape=(
            jax.ShapeDtypeStruct((each, out_cols), BF16),
            jax.ShapeDtypeStruct((seqs, block, per_kv * att), BF16),
            jax.ShapeDtypeStruct((seqs, cols, features), BF16),
        ),
        in_specs=anys + vmems + smems,
        out_specs=[pl.BlockSpec(memory_space=pltpu.VMEM)] * 3,
        scratch_shapes=[
            pltpu.VMEM((seqs, draft, width), BF16),
            pltpu.VMEM((seqs, draft, width), BF16),
            pltpu.VMEM((seqs, draft, state), BF16),
            pltpu.VMEM((seqs, draft, state), BF16),
            pltpu.VMEM((seqs, draft, heads), BF16),
            pltpu.VMEM((seqs, state, width), BF16),
            pltpu.VMEM((seqs, draft, per_kv * att), BF16),
            pltpu.VMEM((seqs, cache, att), BF16),
            pltpu.VMEM((seqs, cache, att), BF16),
            pltpu.VMEM(out_weight.shape, BF16),
            pltpu.VMEM((n_tok, 8, rows), F32),
            pltpu.VMEM((seqs, state, width), BF16),
            pltpu.VMEM((seqs, cols, features), BF16),
            pltpu.VMEM((seqs, per_kv, draft, att), BF16),
            pltpu.VMEM((n_tok, seqs, per_kv, block, att), BF16),
            pltpu.VMEM((n_tok, seqs, per_kv * draft), F32),
            pltpu.VMEM((group, each, out_cols), BF16),
            pltpu.VMEM((group, each, out_cols), BF16),
            pltpu.SemaphoreType.DMA((11, n_tok)),
            pltpu.SemaphoreType.DMA((11, n_tok)),
            pltpu.SemaphoreType.DMA((chunks, group)),
            pltpu.SemaphoreType.DMA((chunks, group)),
            pltpu.SemaphoreType.DMA((10,)),
        ],
        compiler_params=pltpu.CompilerParams(
            collective_id=0, has_side_effects=True, vmem_limit_bytes=48 * 1024 * 1024
        ),
        name="hybrid",
    )(
        mamba_input, gate_input, in_b, in_c, step_size, turned, queries, cached_key_rows,
        cache_values, out_weight, draft_token_keys, draft_values,
        norm_gain.reshape(1, features), decay_rate, skip_weight, cache_len, accepted,
    )
    mamba_out = out.reshape(draft // group, seqs, out_cols)
    committed = jnp.transpose(com.reshape(seqs, cols, heads, size), (0, 2, 3, 1))
    return (mamba_out, ctx, committed)


def solution(mesh):
    in_specs = (
        P("dp", "tok", "head"),
        P("dp", "tok", "head"),
        P("dp", "tok", "head"),
        P("dp", "tok", "head"),
        P("dp", "tok", "head"),
        P("head"),
        P("head"),
        P("head"),
        P("dp", "head", None, "tok"),
        P(("head", "tok"), None),
        P("dp", "tok", "head"),
        P("dp", "tok", "head"),
        P("dp", "tok", "head"),
        P("dp", "tok", "head"),
        P("dp", "tok", "head"),
        P("dp"),
        P("dp"),
    )
    out_specs = (
        P(("head", "tok"), "dp", None),
        P("dp", "tok", "head"),
        P("dp", "head", None, "tok"),
    )
    return jax.shard_map(body, mesh=mesh, in_specs=in_specs, out_specs=out_specs, check_vma=False)
```

time: 130 us -> 48.4 us (0.37)
  waiting for transfers between devices: 46.4 us -> 0 us
  Pallas kernels: 0 us -> 30.5 us
  starting transfers between devices: 20.8 us -> 0 us
  blocking collectives: 17.5 us -> 0 us
  between operations: 14.5 us -> 0.68 us
  matrix products: 10.5 us -> 0 us
  other arithmetic: 5.51 us -> 0 us
  local copies, waits for them, and re-layouts: 14 us -> 16.5 us
    pallas_call x0 -> x1, Pallas kernels: none -> 30.5 us  [body(): pl.pallas_call(functools.partial(kernel, (n_head, n_tok, seqs, block, hea...]
    unnamed x3 -> x0, waiting for transfers between devices: 21.6 us -> none
    all_to_all x6 -> x0, starting transfers between devices: 20.8 us -> none  [the longest x1 4.37 us: body(): lax.all_to_all(in_c, 'tok', split_axis=2, concat_axis=1, tiled=True)]
    reduce_scatter x1 -> x0, waiting for transfers between devices: 18.6 us -> none  [body(): lax.psum_scatter(partial_sum.astype(jnp.bfloat16), 'tok', scatter_dimensi...]
    all_gather x3 -> x0, blocking collectives: 17.5 us -> none  [the longest x1 6.17 us: body(): lax.all_gather(mamba_input, 'tok', axis=1, tiled=True)]
    dot_general x9 -> x0, matrix products: 10.5 us -> none  [the longest x1 2.83 us: body(): jnp.einsum('cmq,czq->cmz', query_matrix, cached_key_rows, preferred_eleme...]
    all_to_all x6 -> x0, waiting for transfers between devices: 6.17 us -> none  [the longest x1 3.28 us: body(): lax.all_to_all(normed, 'tok', split_axis=2, concat_axis=1, tiled=True)]
    unnamed x33, local copies, waits for them, and re-layouts: 7.74 us -> 13.5 us
  transfers between devices with their start and end apart: 8 -> 0, of which waited for: 6 -> 0; matrix products, arithmetic and copies ran while one was open for 16% -> 0% of each run, Pallas kernels for 0% -> 0%
where the time goes in v1:
time: 48.4 us; the launch traced here: 47.7 us
  Pallas kernels  30.5 us (63%)
  local copies, waits for them, and re-layouts  16.5 us (34%)
  between operations  0.68 us (1%)
    pallas_call x1, Pallas kernels, body(): pl.pallas_call(functools.partial(kernel, (n_head, n_tok, seqs, block, hea...  30.5 us
    unnamed x33, local copies, waits for them, and re-layouts  13.5 us
    transpose x1, local copies, waits for them, and re-layouts, body(): jnp.transpose(ssm_state, (0, 3, 1, 2)).reshape(seqs, cols, features)  1.06 us

profile of v1, /device:TPU:0, one launch (start us, length us, event | category | flops | bytes accessed | tf_op | source)
XLA Modules:
  0.0 47.7 jit_solution(3127738752161000897)
XLA Ops:
  0.6 1.1 %copy.20 = bf16[2,32,16,64]{3,2,1,0:T(8,128)(2,1)S(1)} copy(bf16[2,32,16,64]{3,1,2,0:T(8,128)(2,1)} %bitcast.8) | data formatting | bytes 262144 | tf_op jit(solution)/shard_map/transpose | solution.py:318
  1.7 0.2 reshape.18.st_in
  1.9 0.0 copy-start
  1.9 1.6 %copy-done = bf16[256,4096]{1,0:T(8,128)(2,1)S(1)} copy-done((bf16[256,4096]{1,0:T(8,128)(2,1)S(1)}, bf16[256,4096]{1,0:T(8,128)(2,1)}, u32[]{:S(2)}) %copy-start) | copy-done | bytes 2097176
  3.5 0.0 copy-start.1
  3.5 1.0 %copy-done.1 = bf16[2,1024,128]{2,1,0:T(8,128)(2,1)S(1)} copy-done((bf16[2,1024,128]{2,1,0:T(8,128)(2,1)S(1)}, bf16[2,1024,128]{2,1,0:T(8,128)(2,1)}, u32[]{:S(2)}) %copy-start.1) | copy-done | bytes 524312
  4.5 0.0 copy-start.2
  4.5 1.0 %copy-done.2 = bf16[2,1024,128]{2,1,0:T(8,128)(2,1)S(1)} copy-done((bf16[2,1024,128]{2,1,0:T(8,128)(2,1)S(1)}, bf16[2,1024,128]{2,1,0:T(8,128)(2,1)}, u32[]{:S(2)}) %copy-start.2) | copy-done | bytes 524312
  5.6 0.0 copy-start.3
  5.6 0.8 %copy-done.3 = bf16[2,16,1024]{2,1,0:T(8,128)(2,1)S(1)} copy-done((bf16[2,16,1024]{2,1,0:T(8,128)(2,1)S(1)}, bf16[2,16,1024]{2,1,0:T(8,128)(2,1)}, u32[]{:S(2)}) %copy-start.3) | copy-done | bytes 65560
  6.4 0.0 copy-start.4
  6.4 0.8 %copy-done.4 = bf16[2,16,1024]{2,1,0:T(8,128)(2,1)S(1)} copy-done((bf16[2,16,1024]{2,1,0:T(8,128)(2,1)S(1)}, bf16[2,16,1024]{2,1,0:T(8,128)(2,1)}, u32[]{:S(2)}) %copy-start.4) | copy-done | bytes 65560
  7.2 0.0 copy-start.5
  7.2 0.8 %copy-done.5 = bf16[2,16,512]{2,1,0:T(8,128)(2,1)S(1)} copy-done((bf16[2,16,512]{2,1,0:T(8,128)(2,1)S(1)}, bf16[2,16,512]{2,1,0:T(8,128)(2,1)}, u32[]{:S(2)}) %copy-start.5) | copy-done | bytes 32792
  8.0 0.0 copy-start.6
  8.0 0.7 %copy-done.6 = bf16[2,16,128]{2,1,0:T(8,128)(2,1)S(1)} copy-done((bf16[2,16,128]{2,1,0:T(8,128)(2,1)S(1)}, bf16[2,16,128]{2,1,0:T(8,128)(2,1)}, u32[]{:S(2)}) %copy-start.6) | copy-done | bytes 8216
  8.7 0.0 copy-start.7
  8.7 0.7 %copy-done.7 = bf16[2,16,128]{2,1,0:T(8,128)(2,1)S(1)} copy-done((bf16[2,16,128]{2,1,0:T(8,128)(2,1)S(1)}, bf16[2,16,128]{2,1,0:T(8,128)(2,1)}, u32[]{:S(2)}) %copy-start.7) | copy-done | bytes 8216
  9.4 0.0 copy-start.8
  9.4 0.7 %copy-done.8 = bf16[2,16,16]{2,1,0:T(8,128)(2,1)S(1)} copy-done((bf16[2,16,16]{2,1,0:T(8,128)(2,1)S(1)}, bf16[2,16,16]{2,1,0:T(8,128)(2,1)}, u32[]{:S(2)}) %copy-start.8) | copy-done | bytes 1048
  10.1 0.0 copy-start.9
  10.1 0.7 %copy-done.9 = bf16[2,16,128]{2,1,0:T(8,128)(2,1)S(1)} copy-done((bf16[2,16,128]{2,1,0:T(8,128)(2,1)S(1)}, bf16[2,16,128]{2,1,0:T(8,128)(2,1)}, u32[]{:S(2)}) %copy-start.9) | copy-done | bytes 8216
  10.8 0.0 copy-start.10
  10.8 0.7 %copy-done.10 = bf16[2,16,128]{2,1,0:T(8,128)(2,1)S(1)} copy-done((bf16[2,16,128]{2,1,0:T(8,128)(2,1)S(1)}, bf16[2,16,128]{2,1,0:T(8,128)(2,1)}, u32[]{:S(2)}) %copy-start.10) | copy-done | bytes 8216
  11.5 0.0 copy-start.11
  11.5 0.7 %copy-done.11 = f32[1024]{0:T(1024)S(1)} copy-done((f32[1024]{0:T(1024)S(1)}, f32[1024]{0:T(1024)}, u32[]{:S(2)}) %copy-start.11) | copy-done | bytes 4120
  12.2 0.0 copy-start.12
  12.2 0.7 %copy-done.12 = f32[16]{0:T(128)S(1)} copy-done((f32[16]{0:T(128)S(1)}, f32[16]{0:T(128)}, u32[]{:S(2)}) %copy-start.12) | copy-done | bytes 88
  12.8 0.0 copy-start.13
  12.8 0.7 %copy-done.13 = f32[16]{0:T(128)S(1)} copy-done((f32[16]{0:T(128)S(1)}, f32[16]{0:T(128)}, u32[]{:S(2)}) %copy-start.13) | copy-done | bytes 88
  13.5 0.0 copy-start.14
  13.5 0.7 %copy-done.14 = s32[2]{0:T(128)S(1)} copy-done((s32[2]{0:T(128)S(1)}, s32[2]{0:T(128)}, u32[]{:S(2)}) %copy-start.14) | copy-done | bytes 32
  14.1 0.0 copy-start.15
  14.2 0.7 %copy-done.15 = s32[2]{0:T(128)S(1)} copy-done((s32[2]{0:T(128)S(1)}, s32[2]{0:T(128)}, u32[]{:S(2)}) %copy-start.15) | copy-done | bytes 32
  14.8 30.5 %hybrid.1 = (bf16[16,4096]{1,0:T(8,128)(2,1)S(1)}, bf16[2,16,512]{2,1,0:T(8,128)(2,1)S(1)}, bf16[2,32,1024]{2,1,0:T(8,128)(2,1)S(1)}) custom-call(bf16[2,16,1024]{2,1,0:T(8,128)(2,1)S(1)} %copy-done.3, bf16[2,16,1024]{2,1,0:T(8,128)(2,1)S(1)} %copy-done.4, bf16[2,16,128]{2,1,0:T(8,128)(2,1)S(1)} %copy-done.6, bf16[2,16,128]{2,1,0:T(8,128)(2,1)S(1)} %copy-done.7, ...), custom_call_target="tpu_custom_call" | custom-call | tf_op jit(solution)/shard_map/hybrid/pallas_call | solution.py:322
  45.4 0.8 %reshape.20 = bf16[8,2,4096]{2,1,0:T(2,128)(2,1)} reshape(bf16[16,4096]{1,0:T(8,128)(2,1)S(1)} %get-tuple-element.6) | data formatting | bytes 262144 | tf_op jit(solution)/shard_map/reshape | solution.py:365
  46.1 0.2 reshape.21
  46.3 0.8 %copy.23 = bf16[2,32,16,64]{3,1,2,0:T(8,128)(2,1)} copy(bf16[2,32,16,64]{3,2,1,0:T(8,128)(2,1)S(1)} %reshape.21) | data formatting | bytes 262144 | tf_op jit(solution)/shard_map/reshape | solution.py:366
  47.1 0.6 %copy.25 = bf16[2,16,512]{2,1,0:T(8,128)(2,1)} copy(bf16[2,16,512]{2,1,0:T(8,128)(2,1)S(1)} %get-tuple-element.13) | data formatting | bytes 65536
Async XLA Ops:
  1.9 1.6 %copy-start = (bf16[256,4096]{1,0:T(8,128)(2,1)S(1)}, bf16[256,4096]{1,0:T(8,128)(2,1)}, u32[]{:S(2)}) copy-start(bf16[256,4096]{1,0:T(8,128)(2,1)} %w_in.1) | copy-start | bytes 6291460
  3.5 1.0 %copy-start.1 = (bf16[2,1024,128]{2,1,0:T(8,128)(2,1)S(1)}, bf16[2,1024,128]{2,1,0:T(8,128)(2,1)}, u32[]{:S(2)}) copy-start(bf16[2,1024,128]{2,1,0:T(8,128)(2,1)} %k_in.1) | copy-start | bytes 1572868
  4.5 1.0 %copy-start.2 = (bf16[2,1024,128]{2,1,0:T(8,128)(2,1)S(1)}, bf16[2,1024,128]{2,1,0:T(8,128)(2,1)}, u32[]{:S(2)}) copy-start(bf16[2,1024,128]{2,1,0:T(8,128)(2,1)} %v_in.1) | copy-start | bytes 1572868
  5.6 0.8 %copy-start.3 = (bf16[2,16,1024]{2,1,0:T(8,128)(2,1)S(1)}, bf16[2,16,1024]{2,1,0:T(8,128)(2,1)}, u32[]{:S(2)}) copy-start(bf16[2,16,1024]{2,1,0:T(8,128)(2,1)} %x_in.1) | copy-start | bytes 196612
  6.4 0.8 %copy-start.4 = (bf16[2,16,1024]{2,1,0:T(8,128)(2,1)S(1)}, bf16[2,16,1024]{2,1,0:T(8,128)(2,1)}, u32[]{:S(2)}) copy-start(bf16[2,16,1024]{2,1,0:T(8,128)(2,1)} %z_in.1) | copy-start | bytes 196612
  7.2 0.8 %copy-start.5 = (bf16[2,16,512]{2,1,0:T(8,128)(2,1)S(1)}, bf16[2,16,512]{2,1,0:T(8,128)(2,1)}, u32[]{:S(2)}) copy-start(bf16[2,16,512]{2,1,0:T(8,128)(2,1)} %q_in.1) | copy-start | bytes 98308
  8.0 0.7 %copy-start.6 = (bf16[2,16,128]{2,1,0:T(8,128)(2,1)S(1)}, bf16[2,16,128]{2,1,0:T(8,128)(2,1)}, u32[]{:S(2)}) copy-start(bf16[2,16,128]{2,1,0:T(8,128)(2,1)} %b_in.1) | copy-start | bytes 24580
  8.7 0.7 %copy-start.7 = (bf16[2,16,128]{2,1,0:T(8,128)(2,1)S(1)}, bf16[2,16,128]{2,1,0:T(8,128)(2,1)}, u32[]{:S(2)}) copy-start(bf16[2,16,128]{2,1,0:T(8,128)(2,1)} %c_in.1) | copy-start | bytes 24580
  9.4 0.7 %copy-start.8 = (bf16[2,16,16]{2,1,0:T(8,128)(2,1)S(1)}, bf16[2,16,16]{2,1,0:T(8,128)(2,1)}, u32[]{:S(2)}) copy-start(bf16[2,16,16]{2,1,0:T(8,128)(2,1)} %dt_in.1) | copy-start | bytes 3076
  10.1 0.7 %copy-start.9 = (bf16[2,16,128]{2,1,0:T(8,128)(2,1)S(1)}, bf16[2,16,128]{2,1,0:T(8,128)(2,1)}, u32[]{:S(2)}) copy-start(bf16[2,16,128]{2,1,0:T(8,128)(2,1)} %dk_ref.1) | copy-start | bytes 24580
  10.8 0.7 %copy-start.10 = (bf16[2,16,128]{2,1,0:T(8,128)(2,1)S(1)}, bf16[2,16,128]{2,1,0:T(8,128)(2,1)}, u32[]{:S(2)}) copy-start(bf16[2,16,128]{2,1,0:T(8,128)(2,1)} %dv_ref.1) | copy-start | bytes 24580
  11.5 0.7 %copy-start.11 = (f32[1024]{0:T(1024)S(1)}, f32[1024]{0:T(1024)}, u32[]{:S(2)}) copy-start(f32[1024]{0:T(1024)} %param.24) | copy-start | bytes 12292
  12.2 0.7 %copy-start.12 = (f32[16]{0:T(128)S(1)}, f32[16]{0:T(128)}, u32[]{:S(2)}) copy-start(f32[16]{0:T(128)} %rate_ref.1) | copy-start | bytes 196
  12.8 0.7 %copy-start.13 = (f32[16]{0:T(128)S(1)}, f32[16]{0:T(128)}, u32[]{:S(2)}) copy-start(f32[16]{0:T(128)} %skip_ref.1) | copy-start | bytes 196
  13.5 0.7 %copy-start.14 = (s32[2]{0:T(128)S(1)}, s32[2]{0:T(128)}, u32[]{:S(2)}) copy-start(s32[2]{0:T(128)} %len_ref.1) | copy-start | bytes 28
  14.1 0.7 %copy-start.15 = (s32[2]{0:T(128)S(1)}, s32[2]{0:T(128)}, u32[]{:S(2)}) copy-start(s32[2]{0:T(128)} %acc_ref.1) | copy-start | bytes 28

commit v2 on v1

--- a/solution.py
+++ b/solution.py
@@ -26,11 +26,12 @@
 def kernel(
     dims,
     x_in, z_in, b_in, c_in, dt_in, st_in, q_in, k_in, v_in, w_in,
-    dk_ref, dv_ref, gain_ref, rate_ref, skip_ref, len_ref, acc_ref,
+    dk_in, dv_in, gain_in, rate_ref, skip_ref, len_ref, acc_ref,
     out_ref, ctx_ref, com_ref,
     x_l, z_l, b_l, c_l, dt_l, st_l, q_l, k_v, v_v, w_v,
     ss_l, cm_s, cm_l, n_s, n_l, stat_l, part, rs_l,
-    send, recv, rs_send, rs_recv, local,
+    dk_ref, dv_ref, gain_ref, raw_v, turn_v, pair_l, red,
+    send, recv, rs_send, rs_recv, pair_send, pair_recv, local,
 ):
     n_head, n_tok, seqs, block, heads, chunks = dims
     group = n_head * n_tok
@@ -70,11 +71,14 @@
         (b_in, b_l.at[:, mine, :]),
         (c_in, c_l.at[:, mine, :]),
         (dt_in, dt_l.at[:, mine, :]),
-        (st_in.at[:, :, place(tok, width)], st_l.at[:, place(tok, cols), :]),
+        (st_in, raw_v),
         (q_in, q_l.at[:, mine, :]),
         (w_in, w_v),
         (k_in, k_v),
         (v_in, v_v),
+        (dk_in, dk_ref),
+        (dv_in, dv_ref),
+        (gain_in, gain_ref),
     ]
     held = [
         pltpu.make_async_copy(src, dst, local.at[i]) for i, (src, dst) in enumerate(locals_)
@@ -82,6 +86,13 @@
     for copy in held:
         copy.start()
 
+    held[5].wait()
+    for s in range(seqs):
+        turn_v[s] = jnp.concatenate(
+            [raw_v[s, h].astype(F32) for h in range(heads)], axis=1
+        ).astype(BF16)
+    st_l[:, place(tok, cols), :] = turn_v[:, :, place(tok, width)]
+
     pl.semaphore_wait(barrier, group - 1)
 
     def remote(kind, o, src, dst):
@@ -106,7 +117,7 @@
             (b_in, b_l.at[:, mine, :]),
             (c_in, c_l.at[:, mine, :]),
             (x_in.at[:, :, place(to, width)], x_l.at[:, mine, :]),
-            (st_in.at[:, :, place(to, width)], st_l.at[:, place(tok, cols), :]),
+            (turn_v.at[:, :, place(to, width)], st_l.at[:, place(tok, cols), :]),
             (z_in.at[:, :, place(to, width)], z_l.at[:, mine, :]),
         ]
         for kind, (src, dst) in enumerate(pairs):
@@ -115,12 +126,6 @@
     for o in range(1, n_tok):
         ship(6, o, q_in, q_l.at[:, mine, :])
         first[6, o] = started[-1]
-
-    for copy in held[:6]:
-        copy.wait()
-    for kind in range(6):
-        for o in range(1, n_tok):
-            first[kind, o].wait_recv()
 
     lane = iota((1, width), 1)
     rate_x = jnp.zeros((1, width), F32)
@@ -133,6 +138,24 @@
     pick = ((offset >= 0) & (offset < size)).astype(F32).astype(BF16)
     causal = iota((draft, draft), 0) >= iota((draft, draft), 1)
     lower = causal.astype(F32).astype(BF16)
+
+    eye = iota((rows, rows), 0) == iota((rows, rows), 1)
+    source = iota((1, rows), 1)
+    target = jnp.zeros((1, rows), jnp.int32)
+    per = draft // group
+    for s in range(seqs):
+        for g in range(group):
+            start = s * draft + g * per
+            base = (g % 2) * (rows // 2) + (g // 2) * each + s
+            inside = (source >= start) & (source < start + per)
+            target = jnp.where(inside, (source - start) * seqs + base, target)
+    swap = (iota((rows, rows), 0) == target).astype(F32).astype(BF16)
+
+    for copy in held[:5]:
+        copy.wait()
+    for kind in range(6):
+        for o in range(1, n_tok):
+            first[kind, o].wait_recv()
 
     gated = []
     saved = []
@@ -152,7 +175,6 @@
         saved.append((x, dtx, run))
     gated = jnp.concatenate(gated, axis=0)
     sums = jnp.sum(gated * gated, axis=1, keepdims=True)
-    eye = iota((rows, rows), 0) == iota((rows, rows), 1)
     sum_row = jnp.sum(jnp.where(eye, sums, 0.0), axis=0, keepdims=True)
     ss_l[tok] = jnp.broadcast_to(sum_row, (8, rows))
     for o in range(1, n_tok):
@@ -174,40 +196,62 @@
     for t in range(n_tok):
         totals = totals + ss_l[t][0:1, :]
     col = jnp.sum(jnp.where(eye, totals, 0.0), axis=1, keepdims=True)
+    held[12].wait()
     gain = gain_ref[:, place(tok, width)]
     normed = gated * lax.rsqrt(col / (width * n_tok) + EPSILON) * gain
-    swap = None
-    for s in range(seqs):
-        k = iota((rows, rows), 1) - s * draft
-        hit = (k >= 0) & (k < draft) & (k * seqs + s == iota((rows, rows), 0))
-        swap = hit if swap is None else swap | hit
-    normed = dot(swap.astype(F32).astype(BF16), normed.astype(BF16)).astype(BF16)
+    normed = dot(swap, normed.astype(BF16)).astype(BF16)
 
     held[7].wait()
     tile = min(512, span)
     rs = {}
-    for ch in range(chunks):
-        for start in range(ch * span, (ch + 1) * span, tile):
-            val = dot(normed, w_v[:, start : start + tile]).astype(BF16)
-            for g in range(group):
-                part[g, :, start : start + tile] = val[g * each : (g + 1) * each]
-        for o in range(1, group):
-            peer = lax.rem(me + o, group)
-            piece = pl.ds(ch * span, span)
+    pairs = []
+    half = group // 2
+    side = lax.rem(tok, 2)
+    lines = n_tok // 2
+    slot = head * lines + tok // 2
+
+    def forward(ch):
+        pairs[ch].wait_recv()
+        piece = pl.ds(ch * span, span)
+        red[:, :, piece] = (
+            part[side, :, :, piece].astype(F32) + pair_l[:, :, piece].astype(F32)
+        ).astype(BF16)
+        for o in range(1, half):
+            peer = lax.rem(slot + o, half)
             copy = pltpu.make_async_remote_copy(
-                src_ref=part.at[peer, :, piece], dst_ref=rs_l.at[o, :, piece],
+                src_ref=red.at[peer, :, piece], dst_ref=rs_l.at[o, :, piece],
                 send_sem=rs_send.at[ch, o], recv_sem=rs_recv.at[ch, o],
-                device_id={"head": peer // n_tok, "tok": lax.rem(peer, n_tok)},
+                device_id={"head": peer // lines, "tok": lax.rem(peer, lines) * 2 + side},
                 device_id_type=MESH,
             )
             copy.start()
             rs[ch, o] = copy
 
+    for ch in range(chunks):
+        for start in range(ch * span, (ch + 1) * span, tile):
+            val = dot(normed, w_v[:, start : start + tile]).astype(BF16)
+            for p in range(2):
+                for g in range(half):
+                    at = (p * half + g) * each
+                    part[p, g, :, start : start + tile] = val[at : at + each]
+        piece = pl.ds(ch * span, span)
+        copy = pltpu.make_async_remote_copy(
+            src_ref=part.at[1 - side, :, :, piece], dst_ref=pair_l.at[:, :, piece],
+            send_sem=pair_send.at[ch], recv_sem=pair_recv.at[ch],
+            device_id={"tok": tok + 1 - 2 * side}, device_id_type=MESH,
+        )
+        copy.start()
+        pairs.append(copy)
+        if ch > 0:
+            forward(ch - 1)
+    forward(chunks - 1)
+
     for o in range(1, n_tok):
         first[6, o].wait_recv()
     held[6].wait()
     held[8].wait()
-    held[9].wait()
+    for copy in held[9:12]:
+        copy.wait()
     scale = att ** (-0.5)
     m_rows = per_kv * draft
     big = iota((m_rows, m_rows), 0) == iota((m_rows, m_rows), 1)
@@ -249,11 +293,11 @@
     cm_l[:, :, place(tok, width)] = cm_s[:, place(tok, cols), :]
 
     for ch in range(chunks):
-        for o in range(1, group):
+        for o in range(1, half):
             rs[ch, o].wait_recv()
         for start in range(ch * span, (ch + 1) * span, tile):
-            acc = part[me, :, start : start + tile].astype(F32)
-            for o in range(1, group):
+            acc = red[slot, :, start : start + tile].astype(F32)
+            for o in range(1, half):
                 acc = acc + rs_l[o, :, start : start + tile].astype(F32)
             out_ref[:, start : start + tile] = acc.astype(BF16)
 
@@ -286,10 +330,12 @@
 
     for o in range(1, n_tok):
         first[10, o].wait_recv()
-    com_ref[...] = cm_l[...]
+    for s in range(seqs):
+        for h in range(heads):
+            com_ref[s, h] = cm_l[s, :, h * size : (h + 1) * size]
     for copy in started:
         copy.wait_send()
-    for copy in rs.values():
+    for copy in pairs + list(rs.values()):
         copy.wait_send()
 
 
@@ -314,19 +360,19 @@
     out_cols = out_weight.shape[1]
     rows = seqs * draft
     each = rows // group
-    chunks = 2
-    turned = jnp.transpose(ssm_state, (0, 3, 1, 2)).reshape(seqs, cols, features)
-    anys = [pl.BlockSpec(memory_space=pl.ANY)] * 10
-    vmems = [pl.BlockSpec(memory_space=pltpu.VMEM)] * 3
+    chunks = 4
+    half = group // 2
+    turned = jnp.transpose(ssm_state, (0, 1, 3, 2))
+    anys = [pl.BlockSpec(memory_space=pl.ANY)] * 13
     smems = [pl.BlockSpec(memory_space=pltpu.SMEM)] * 4
     out, ctx, com = pl.pallas_call(
         functools.partial(kernel, (n_head, n_tok, seqs, block, heads, chunks)),
         out_shape=(
             jax.ShapeDtypeStruct((each, out_cols), BF16),
             jax.ShapeDtypeStruct((seqs, block, per_kv * att), BF16),
-            jax.ShapeDtypeStruct((seqs, cols, features), BF16),
+            jax.ShapeDtypeStruct((seqs, heads, cols, size), BF16),
         ),
-        in_specs=anys + vmems + smems,
+        in_specs=anys + smems,
         out_specs=[pl.BlockSpec(memory_space=pltpu.VMEM)] * 3,
         scratch_shapes=[
             pltpu.VMEM((seqs, draft, width), BF16),
@@ -345,16 +391,25 @@
             pltpu.VMEM((seqs, per_kv, draft, att), BF16),
             pltpu.VMEM((n_tok, seqs, per_kv, block, att), BF16),
             pltpu.VMEM((n_tok, seqs, per_kv * draft), F32),
-            pltpu.VMEM((group, each, out_cols), BF16),
-            pltpu.VMEM((group, each, out_cols), BF16),
+            pltpu.VMEM((2, half, each, out_cols), BF16),
+            pltpu.VMEM((half, each, out_cols), BF16),
+            pltpu.VMEM((seqs, block, att), BF16),
+            pltpu.VMEM((seqs, block, att), BF16),
+            pltpu.VMEM((1, features), F32),
+            pltpu.VMEM((seqs, heads, cols, size), BF16),
+            pltpu.VMEM((seqs, cols, features), BF16),
+            pltpu.VMEM((half, each, out_cols), BF16),
+            pltpu.VMEM((half, each, out_cols), BF16),
             pltpu.SemaphoreType.DMA((11, n_tok)),
             pltpu.SemaphoreType.DMA((11, n_tok)),
-            pltpu.SemaphoreType.DMA((chunks, group)),
-            pltpu.SemaphoreType.DMA((chunks, group)),
-            pltpu.SemaphoreType.DMA((10,)),
+            pltpu.SemaphoreType.DMA((chunks, half)),
+            pltpu.SemaphoreType.DMA((chunks, half)),
+            pltpu.SemaphoreType.DMA((chunks,)),
+            pltpu.SemaphoreType.DMA((chunks,)),
+            pltpu.SemaphoreType.DMA((13,)),
         ],
         compiler_params=pltpu.CompilerParams(
-            collective_id=0, has_side_effects=True, vmem_limit_bytes=48 * 1024 * 1024
+            collective_id=0, has_side_effects=True, vmem_limit_bytes=67043328
         ),
         name="hybrid",
     )(
@@ -363,7 +418,7 @@
         norm_gain.reshape(1, features), decay_rate, skip_weight, cache_len, accepted,
     )
     mamba_out = out.reshape(draft // group, seqs, out_cols)
-    committed = jnp.transpose(com.reshape(seqs, cols, heads, size), (0, 2, 3, 1))
+    committed = jnp.transpose(com, (0, 1, 3, 2))
     return (mamba_out, ctx, committed)
 
 

time: 48.4 us -> 32.9 us (0.68); the launches traced: 47.7 us -> 32.7 us
  local copies, waits for them, and re-layouts: 16.5 us -> 4.71 us
  Pallas kernels: 30.5 us -> 27.3 us
    unnamed x33 -> x2, local copies, waits for them, and re-layouts: 13.5 us -> 3.04 us
    pallas_call x1, Pallas kernels: 30.5 us -> 27.3 us  [body(): pl.pallas_call(functools.partial(kernel, (n_head, n_tok, seqs, block, hea...]
    reshape x3 -> x0, local copies, waits for them, and re-layouts: 1.15 us -> none  [the longest x2 0.95 us: body(): com.reshape(seqs, cols, heads, size)]
    transpose x1 -> x0, local copies, waits for them, and re-layouts: 1.06 us -> none  [body(): jnp.transpose(ssm_state, (0, 3, 1, 2)).reshape(seqs, cols, features)]
    reshape x1, local copies, waits for them, and re-layouts: 0.76 us -> 1.67 us  [body(): mamba_out = out.reshape(draft // group, seqs, out_cols)]
where the time goes in v2:
time: 32.9 us; the launch traced here: 32.7 us
  Pallas kernels  27.3 us (83%)
  local copies, waits for them, and re-layouts  4.71 us (14%)
  between operations  0.65 us (2%)
    pallas_call x1, Pallas kernels, body(): pl.pallas_call(functools.partial(kernel, (n_head, n_tok, seqs, block, hea...  27.3 us
    unnamed x2, local copies, waits for them, and re-layouts  3.04 us
    reshape x1, local copies, waits for them, and re-layouts, body(): mamba_out = out.reshape(draft // group, seqs, out_cols)  1.67 us

profile of v2, /device:TPU:0, one launch (start us, length us, event | category | flops | bytes accessed | tf_op | source)
XLA Modules:
  0.0 32.7 jit_solution(2454730275662589437)
XLA Ops:
  0.6 27.3 %hybrid.1 = (bf16[16,4096]{1,0:T(8,128)(2,1)}, bf16[2,16,512]{2,1,0:T(8,128)(2,1)}, bf16[2,16,32,64]{3,2,1,0:T(8,128)(2,1)}) custom-call(bf16[2,16,1024]{2,1,0:T(8,128)(2,1)} %x_in.1, bf16[2,16,1024]{2,1,0:T(8,128)(2,1)} %z_in.1, bf16[2,16,128]{2,1,0:T(8,128)(2,1)} %b_in.1, bf16[2,16,128]{2,1,0:T(8,128)(2,1)} %c_in.1, bf16[2,16,16]{2,1,0:T(8,128)(2,1)} %dt_in.1, ...), custom_call_target="tpu_custom_call" | custom-call | tf_op jit(solution)/shard_map/hybrid/pallas_call | solution.py:368
  28.0 1.7 %reshape.13 = bf16[8,2,4096]{2,1,0:T(2,128)(2,1)} reshape(bf16[16,4096]{1,0:T(8,128)(2,1)} %get-tuple-element.6) | data formatting | bytes 262144 | tf_op jit(solution)/shard_map/reshape | solution.py:420
  29.7 1.4 %copy.22 = bf16[2,16,512]{2,1,0:T(8,128)(2,1)} copy(bf16[2,16,512]{2,1,0:T(8,128)(2,1)} %get-tuple-element.13) | data formatting | bytes 65536
  31.0 1.7 %copy.23 = bf16[2,16,64,32]{2,3,1,0:T(8,128)(2,1)} copy(bf16[2,16,64,32]{2,3,1,0:T(8,128)(2,1)} %bitcast.3) | data formatting | bytes 262144
